TPU v7x, 32 devices: a whole 2x2x4 slice. The times are simulated.
32 devices in a mesh: section: 4 (over x, core), dp: 8 (over z, y).
Axes of the slice: x: 2, y: 2, z: 4, core: 2. Of those that a mesh axis runs over, the one named last changes fastest.
Arguments:
- student_states: bfloat16 [64, 512, 1024], P('dp'), may hold values from -6 to 6
- lengths: int32 [64], P('dp'), may hold values from 64 to 512
- student_ln_gain: float32 [1024], replicated, may hold values from 0.1 to 1.9
- student_w_in: bfloat16 [1024, 4096], P(None, 'section'), may hold values from -0.1875 to 0.1875
- student_w_out: bfloat16 [4096, 1024], P('section'), may hold values from -0.09375 to 0.09375
- teacher_rows: bfloat16 [64, 4096], P('dp'), may hold values from -6 to 6
- teacher_mlp_gain: float32 [4096], replicated, may hold values from 0.1 to 1.9
- teacher_gate_up: bfloat16 [2, 4096, 12288], P(None, 'dp', 'section'), may hold values from -0.09375 to 0.09375
- teacher_down: bfloat16 [12288, 4096], P('section', 'dp'), may hold values from -0.0546875 to 0.0546875
- teacher_final_gain: float32 [4096], replicated, may hold values from 0.1 to 1.9
Outputs:
- loss: float32 [], replicated
- grad_w_in: float32 [1024, 4096], P('dp', 'section')
- grad_w_out: float32 [4096, 1024], P(('section', 'dp'))
- teacher_states: float32 [64, 4096], P('dp', 'section')
Inputs may be any that keep to these rules, and one draw needn't show every extreme that they name: Each document's first lengths tokens are real, the rest padding.
All inputs are finite; a program needn't handle non-finite values.
Results may differ from a plain program's by a relative error of at most 0.013.
The roundings to bfloat16 on the way count: a program that leaves them out, or rounds other values in their place, can miss the bound.
Values may be sent and summed in bfloat16 or wider, within the bound.
No kernel may reach another device: no remote copies, remote signals or barrier semaphores. Data moves between devices by JAX's collectives and lax.ppermute only.
A program may use at most 128 MiB of HBM per device.

v0:
```python
import jax
import jax.numpy as jnp
from jax import lax
from jax.sharding import PartitionSpec as P

student_softness = 0.05
teacher_softness = 0.02


def layer_norm(states, gain):
    values = states.astype(jnp.float32)
    center = values - jnp.mean(values, -1, keepdims=True)
    spread = jnp.mean(center * center, -1, keepdims=True)
    return (center * lax.rsqrt(spread + 1e-05) * gain).astype(jnp.bfloat16)


def gelu_exact(value):
    return 0.5 * value * (1.0 + jax.scipy.special.erf(value * 0.7071067811865476))


def gelu_slope(value):
    return (
        0.5 * (1.0 + jax.scipy.special.erf(value * 0.7071067811865476))
        + value * jnp.exp(-0.5 * value * value) * 0.3989422804014327
    )


def contrast(student_logits, teacher_logits, row_ids, col_ids):
    keep = row_ids[:, None] != col_ids[None, :]
    partner = (row_ids + 1 - 2 * (row_ids % 2))[:, None] == col_ids[None, :]
    s_exp = jnp.where(keep, jnp.exp(student_logits), 0.0)
    t_exp = jnp.where(keep, jnp.exp(teacher_logits), 0.0)
    s_total = jnp.sum(s_exp, -1, keepdims=True)
    t_total = jnp.sum(t_exp, -1, keepdims=True)
    s_prob = s_exp / s_total
    t_prob = t_exp / t_total
    s_log = student_logits - jnp.log(s_total)
    t_log = teacher_logits - jnp.log(t_total)
    terms = jnp.where(partner, -s_log, 0.0) + jnp.where(keep, t_prob * (t_log - s_log), 0.0)
    gradient_list = 2.0 * s_prob - partner.astype(jnp.float32) - t_prob
    return (gradient_list, jnp.sum(terms))


def on_device(
    student_states,
    lengths,
    student_ln_gain,
    student_w_in,
    student_w_out,
    teacher_rows,
    teacher_mlp_gain,
    teacher_gate_up,
    teacher_down,
    teacher_final_gain,
):
    dp_count = lax.axis_size("dp")
    dp_index = lax.axis_index("dp")
    section_index = lax.axis_index("section")
    local_docs = teacher_rows.shape[0]
    total_docs = local_docs * dp_count
    highest_precision = lax.Precision.HIGHEST
    rows_f = teacher_rows.astype(jnp.float32)
    inverse = lax.rsqrt(jnp.mean(rows_f * rows_f, -1, keepdims=True) + 1e-06)
    normed = (rows_f * inverse * teacher_mlp_gain).astype(jnp.bfloat16)
    col_width = teacher_gate_up.shape[1]
    hidden_width = teacher_gate_up.shape[2]
    every_row = lax.all_gather(normed, "dp", axis=0, tiled=True)
    columns = lax.dynamic_slice_in_dim(every_row, dp_index * col_width, col_width, 1)
    gate_part = jnp.dot(columns, teacher_gate_up[0], preferred_element_type=jnp.float32)
    upper_part = jnp.dot(columns, teacher_gate_up[1], preferred_element_type=jnp.float32)
    both = lax.psum_scatter(
        jnp.concatenate([gate_part, upper_part], axis=1), "dp", scatter_dimension=0, tiled=True
    )
    hidden = (jax.nn.silu(both[:, :hidden_width]) * both[:, hidden_width:]).astype(jnp.bfloat16)
    partial_out = jnp.dot(
        lax.all_gather(hidden, "dp", axis=0, tiled=True),
        teacher_down,
        preferred_element_type=jnp.float32,
    )
    per_doc = lax.all_to_all(partial_out, "dp", split_axis=0, concat_axis=1, tiled=True)
    mlp_part = lax.psum_scatter(per_doc, "section", scatter_dimension=1, tiled=True)
    part_width = mlp_part.shape[1]
    teacher_states = (
        lax.dynamic_slice_in_dim(rows_f, section_index * part_width, part_width, 1) + mlp_part
    )
    final_gain = lax.dynamic_slice_in_dim(
        teacher_final_gain, section_index * part_width, part_width, 0
    )
    scaled = teacher_states * final_gain
    teacher_square = jnp.sum(scaled * scaled, -1)
    seq_len = student_states.shape[1]
    width = student_states.shape[2]
    tokens = layer_norm(student_states, student_ln_gain).reshape(local_docs * seq_len, width)
    pre_act = jnp.dot(tokens, student_w_in, preferred_element_type=jnp.float32)
    act = gelu_exact(pre_act).astype(jnp.bfloat16).reshape(local_docs, seq_len, -1)
    positions = jnp.arange(seq_len, dtype=jnp.int32)
    mask_f = (positions[None, :] < lengths[:, None]).astype(jnp.float32)
    mask_low = mask_f.astype(jnp.bfloat16)
    counts = lengths.astype(jnp.float32)[:, None]
    pooled_act = (
        jnp.einsum("bs,bsf->bf", mask_low, act, preferred_element_type=jnp.float32) / counts
    ).astype(jnp.bfloat16)
    pooled_x = (
        jnp.einsum("bs,bse->be", mask_low, student_states, preferred_element_type=jnp.float32)
        / counts
    )
    partial_emb = jnp.dot(pooled_act, student_w_out, preferred_element_type=jnp.float32)
    emb_sum, teacher_total = lax.psum((partial_emb, teacher_square), "section")
    student_raw = pooled_x + emb_sum
    norms = jnp.sqrt(jnp.sum(student_raw * student_raw, -1, keepdims=True) + 1e-06)
    student_normalized = student_raw / norms
    teacher_normalized = scaled / jnp.sqrt(teacher_total[:, None] + 1e-06)
    all_student_rows, every_teacher = (
        lax.all_gather(student_normalized, "dp", axis=0, tiled=True),
        lax.all_gather(teacher_normalized, "dp", axis=0, tiled=True),
    )
    first_row = dp_index * local_docs
    col_ids = jnp.arange(total_docs, dtype=jnp.int32)
    teacher_gram = lax.psum(
        jnp.dot(every_teacher, every_teacher.T, precision=highest_precision), "section"
    )
    teacher_logits = teacher_gram / teacher_softness
    student_logits = (
        jnp.dot(all_student_rows, all_student_rows.T, precision=highest_precision)
        / student_softness
    )
    gradient_list, loss = contrast(student_logits, teacher_logits, col_ids, col_ids)
    symmetric = (
        lax.dynamic_slice_in_dim(gradient_list, first_row, local_docs, 0)
        + lax.dynamic_slice_in_dim(gradient_list, first_row, local_docs, 1).T
    )
    normalized_gradient = (
        jnp.dot(symmetric, all_student_rows, precision=highest_precision) / student_softness
    )
    raw_grad = (
        normalized_gradient
        - student_normalized * jnp.sum(student_normalized * normalized_gradient, -1, keepdims=True)
    ) / norms
    raw_low = raw_grad.astype(jnp.bfloat16)
    grad_out_part = jnp.dot(pooled_act.T, raw_low, preferred_element_type=jnp.float32)
    pool_grad = lax.dot_general(
        raw_low, student_w_out, (((1,), (1,)), ((), ())), preferred_element_type=jnp.float32
    )
    scale = pool_grad / counts
    slope = gelu_slope(pre_act).reshape(local_docs, seq_len, -1)
    act_grad = (
        (slope * mask_f[:, :, None] * scale[:, None, :])
        .astype(jnp.bfloat16)
        .reshape(local_docs * seq_len, -1)
    )
    grad_w_in = lax.psum_scatter(
        lax.dot_general(
            tokens, act_grad, (((0,), (0,)), ((), ())), preferred_element_type=jnp.float32
        ),
        "dp",
        scatter_dimension=0,
        tiled=True,
    )
    grad_w_out = lax.psum_scatter(grad_out_part, "dp", scatter_dimension=0, tiled=True)
    return (loss, grad_w_in, grad_w_out, teacher_states)


def solution(mesh):
    placed = (
        P("dp", None, None),
        P("dp"),
        P(),
        P(None, "section"),
        P("section", None),
        P("dp", None),
        P(),
        P(None, "dp", "section"),
        P("section", "dp"),
        P(),
    )
    return jax.shard_map(
        on_device,
        mesh=mesh,
        in_specs=placed,
        out_specs=(P(), P("dp", "section"), P(("section", "dp"), None), P("dp", "section")),
        check_vma=False,
    )
```

profile of v0, /device:TPU:0, one launch (start us, length us, event | category | flops | bytes accessed | tf_op | source)
XLA Modules:
  0.0 472.4 jit_solution(15966292794362974652)
XLA Ops:
  7.2 0.0 copy-start
  7.2 0.0 reduce-scatter.5.cloned.1.call-start
  7.2 1.1 multiply_reduce_fusion
  8.4 0.9 multiply_convert_fusion.5
  9.3 35.3 %all_gather.13 = bf16[64,4096]{1,0:T(8,128)(2,1)} all-gather(bf16[8,4096]{1,0:T(8,128)(2,1)S(1)} %multiply_convert_fusion.5), channel_id=1, replica_groups=mesh['section'=4,'dp'=8] {'dp'}, dimensions={0}, use_global_device_ids=true | all-gather | bytes 589824 | tf_op jit(solution)/shard_map/all_gather | solution.py:67
  44.6 2.6 fusion.12
  47.2 2.6 fusion.14
  49.8 1.3 pad_maximum_fusion
  51.0 0.0 reduce-scatter.5.cloned.1.call-update
  51.1 0.0 copy-start.7
  51.1 0.0 slice-start
  51.1 0.0 copy-start.6
  51.1 4.7 convert_reduce_fusion
  55.8 0.0 slice-start.1
  55.8 5.7 %fusion.2 = f32[8,512]{1,0:T(8,128)S(1)} fusion(bf16[8,512,1024]{2,1,0:T(8,128)(2,1)} %param.10, f32[8,512]{1,0:T(8,128)S(1)} %broadcast_multiply_fusion), kind=kLoop, calls=%fused_computation.5 | loop fusion | flops 16773120 | bytes 8421376 | tf_op jit(solution)/shard_map/reduce_sum | solution.py:13
  61.6 0.0 copy-done.7
  61.6 0.7 fusion.27
  62.2 0.0 copy-done.6
  62.2 2.8 fusion.4
  65.1 0.0 copy-start.8
  65.1 1.2 fusion.30
  66.3 2.4 copy-done.1
  68.7 0.0 copy-done.8
  68.7 16.7 %fusion.8 = (f32[4096,1024]{1,0:T(8,128)}, bf16[4096,1024]{1,0:T(8,128)(2,1)}) fusion(bf16[4096,1024]{1,0:T(8,128)(2,1)S(1)} %bitcast.56, bf16[1024,1024]{1,0:T(8,128)(2,1)S(1)} %copy-done.8), kind=kOutput, calls=%fused_computation.11 | convolution fusion | flops 8636071936 | bytes 35651584 | tf_op jit(solution)/shard_map/dot_general | solution.py:94
  85.3 32.8 %reduce-scatter.5.cloned.1.call-done = f32[8,6144]{1,0:T(8,128)} async-done(((f32[64,6144]{1,0:T(8,128)}), f32[8,6144]{1,0:T(8,128)}) %reduce-scatter.5.cloned.1.call-update) | async-done | bytes 196624 | tf_op jit(solution)/shard_map/reduce_scatter | solution.py:71
  118.1 1.0 fusion.19
  119.1 31.0 %all_gather.14 = bf16[64,3072]{1,0:T(8,128)(2,1)S(1)} all-gather(bf16[8,3072]{1,0:T(8,128)(2,1)S(1)} %fusion.19), channel_id=1, replica_groups=mesh['section'=4,'dp'=8] {'dp'}, dimensions={0}, use_global_device_ids=true | all-gather | bytes 442368 | tf_op jit(solution)/shard_map/all_gather | solution.py:76
  150.1 1.3 convolution_bitcast_fusion
  151.4 3.4 all-to-all-start
  154.8 0.0 reduce-scatter.7.cloned.1.call-start
  154.9 4.6 fusion.28
  159.4 0.0 copy-done.2
  159.4 0.7 convert_element_type.50
  160.1 0.7 dynamic_slice.17
  160.8 1.3 all-to-all-done
  162.1 0.7 copy-done.3
  162.7 0.0 reduce-scatter.7.cloned.1.call-update
  162.8 0.0 reduce-scatter.9.cloned.1.call-start
  162.8 2.0 fusion.40
  164.8 17.8 %reduce-scatter.7.cloned.1.call-done = f32[8,1024]{1,0:T(8,128)} async-done(((f32[8,4096]{1,0:T(8,128)}), f32[8,1024]{1,0:T(8,128)}) %reduce-scatter.7.cloned.1.call-update) | async-done | bytes 32784 | tf_op jit(solution)/shard_map/reduce_scatter | solution.py:81
  182.6 0.9 multiply_reduce_fusion.2
  183.5 5.8 %psum.22 = f32[8]{0:T(128)S(1)} all-reduce(f32[8]{0:T(128)S(1)} %get-tuple-element.6), channel_id=1, replica_groups=mesh['section'=4,'dp'=8] {'section'}, use_global_device_ids=true, to_apply=%region_9.10 | all-reduce | flops 8 | bytes 64 | tf_op jit(solution)/shard_map/psum | solution.py:108
  189.3 0.1 multiply_divide_fusion
  189.3 31.1 %all_gather.15 = f32[64,1024]{1,0:T(8,128)S(1)} all-gather(f32[8,1024]{1,0:T(8,128)S(1)} %multiply_divide_fusion), channel_id=1, replica_groups=mesh['section'=4,'dp'=8] {'dp'}, dimensions={0}, use_global_device_ids=true | all-gather | bytes 294912 | tf_op jit(solution)/shard_map/all_gather | solution.py:115
  220.5 0.4 fusion.42
  220.9 11.1 %all-reduce = (f32[8,1024]{1,0:T(8,128)S(1)}, f32[64,64]{0,1:T(8,128)S(1)}) all-reduce(f32[8,1024]{1,0:T(8,128)S(1)} %fusion.40, f32[64,64]{0,1:T(8,128)S(1)} %fusion.42), channel_id=1, replica_groups=mesh['section'=4,'dp'=8] {'section'}, use_global_device_ids=true, to_apply=%region_2.3 | all-reduce | flops 12288 | bytes 98304 | tf_op jit(solution)/shard_map/psum | solution.py:108
  232.0 0.0 copy-start.5
  232.0 0.2 multiply_reduce_fusion.3
  232.2 0.1 broadcast_divide_fusion
  232.3 30.9 %all_gather.12 = f32[64,1024]{1,0:T(8,128)S(1)} all-gather(f32[8,1024]{1,0:T(8,128)S(1)} %broadcast_divide_fusion), channel_id=1, replica_groups=mesh['section'=4,'dp'=8] {'dp'}, dimensions={0}, use_global_device_ids=true | all-gather | bytes 294912 | tf_op jit(solution)/shard_map/all_gather | solution.py:114
  263.2 0.4 fusion.24
  263.7 1.4 subtract_subtract_fusion
  265.1 0.7 constant_dynamic-slice_fusion
  265.8 0.8 copy.22
  266.6 0.4 multiply_reduce_fusion.1
  266.9 0.1 divide_convert_fusion
  267.0 2.2 convolution_divide_fusion
  269.3 16.3 %fusion.18 = f32[1024,1024]{1,0:T(8,128)} fusion(bf16[8,512,1024]{2,1,0:T(8,128)(2,1)} %copy-done.1, f32[8,512,1024]{2,1,0:T(8,128)} %bitcast.58, f32[8,1024]{1,0:T(8,128)S(1)} %convolution_divide_fusion, f32[8,512]{1,0:T(8,128)} %get-tuple-element.12), kind=kOutput, calls=%fused_computation.24 | convolution fusion | flops 8602517504 | bytes 29409280 | tf_op jit(solution)/shard_map/dot_general | solution.py:152
  285.6 0.0 reduce-scatter.9.cloned.1.call-update
  285.6 0.0 reduce-scatter.11.cloned.1.call-start
  285.6 2.7 fusion.38
  288.4 0.0 reduce-scatter.11.cloned.1.call-update
  288.4 85.4 %reduce-scatter.9.cloned.1.call-done = f32[128,1024]{1,0:T(8,128)} async-done(((f32[1024,1024]{1,0:T(8,128)}), f32[128,1024]{1,0:T(8,128)}) %reduce-scatter.9.cloned.1.call-update) | async-done | bytes 524304 | tf_op jit(solution)/shard_map/reduce_scatter | solution.py:151
  373.8 92.1 %reduce-scatter.11.cloned.1.call-done = f32[128,1024]{1,0:T(8,128)} async-done(((f32[1024,1024]{1,0:T(8,128)}), f32[128,1024]{1,0:T(8,128)}) %reduce-scatter.11.cloned.1.call-update) | async-done | bytes 524304 | tf_op jit(solution)/shard_map/reduce_scatter | solution.py:159
  (20 shorter events, 0.1 us)
Async XLA Ops:
  7.2 142.9 %copy-start = (bf16[3072,512]{1,0:T(8,128)(2,1)S(1)}, bf16[3072,512]{1,0:T(8,128)(2,1)}, u32[]{:S(2)}) copy-start(bf16[3072,512]{1,0:T(8,128)(2,1)} %param.18) | copy-start | bytes 9437188
  7.2 110.9 %reduce-scatter.5.cloned.1.call-start = ((), (), s32[]{:S(2)}) async-start(), calls=%async_computation.5 | async-start | bytes 1769472 | tf_op jit(solution)/shard_map/reduce_scatter | solution.py:71
  51.1 10.5 %copy-start.7 = (s32[8]{0:T(128)S(1)}, s32[8]{0:T(128)}, u32[]{:S(2)}) copy-start(s32[8]{0:T(128)} %param.11) | copy-start | bytes 100
  51.1 11.2 %slice-start = ((s8[8388608]{0:T(1024)(128)(4,1)}), s8[4194304]{0:T(1024)(128)(4,1)S(1)}, s32[]{:S(2)}) async-start(s8[8388608]{0:T(1024)(128)(4,1)} %bitcast.53), calls=%async_computation.9 | async-start | bytes 8388608
  51.1 11.2 %copy-start.6 = (f32[1024]{0:T(1024)S(1)}, f32[1024]{0:T(1024)}, u32[]{:S(2)}) copy-start(f32[1024]{0:T(1024)} %param.12) | copy-start | bytes 12292
  55.8 6.4 %slice-start.1 = ((s8[8388608]{0:T(1024)(128)(4,1)}), s8[4194304]{0:T(1024)(128)(4,1)S(1)}, s32[]{:S(2)}) async-start(s8[8388608]{0:T(1024)(128)(4,1)} %bitcast.53), calls=%async_computation.10 | async-start | bytes 8388608
  65.1 3.6 copy-start.1
  65.1 3.6 copy-start.8
  85.3 74.1 %copy-start.2 = (bf16[8,4096]{1,0:T(8,128)(2,1)S(1)}, bf16[8,4096]{1,0:T(8,128)(2,1)}, u32[]{:S(2)}) copy-start(bf16[8,4096]{1,0:T(8,128)(2,1)} %param.15) | copy-start | bytes 196612
  151.4 10.7 %all-to-all-start = ((f32[8,8,512]{2,1,0:T(8,128)}), f32[8,8,512]{2,1,0:T(8,128)S(1)}, u32[]{:S(2)}, u32[]{:S(2)}) async-start(f32[8,8,512]{2,1,0:T(8,128)} %convolution_bitcast_fusion), calls=%async_computation.1 | async-start | bytes 262144 | tf_op jit(solution)/shard_map/all_to_all | solution.py:80
  154.8 27.8 %reduce-scatter.7.cloned.1.call-start = ((), (), s32[]{:S(2)}) async-start(), calls=%async_computation.6 | async-start | bytes 163840 | tf_op jit(solution)/shard_map/reduce_scatter | solution.py:81
  162.1 0.7 copy-start.3
  162.8 211.0 %reduce-scatter.9.cloned.1.call-start = ((), (), s32[]{:S(2)}) async-start(), calls=%async_computation.7 | async-start | bytes 4718592 | tf_op jit(solution)/shard_map/reduce_scatter | solution.py:151
  183.5 102.1 %copy-start.4 = (f32[8,1024]{1,0:T(8,128)}, f32[8,1024]{1,0:T(8,128)S(1)}, u32[]{:S(2)}) copy-start(f32[8,1024]{1,0:T(8,128)S(1)} %get-tuple-element.7) | copy-start | bytes 98308
  232.0 31.7 %copy-start.5 = (f32[64,64]{0,1:T(8,128)}, f32[64,64]{0,1:T(8,128)S(1)}, u32[]{:S(2)}) copy-start(f32[64,64]{0,1:T(8,128)S(1)} %get-tuple-element.5) | copy-start | bytes 49156
  285.6 180.3 %reduce-scatter.11.cloned.1.call-start = ((), (), s32[]{:S(2)}) async-start(), calls=%async_computation.8 | async-start | bytes 4718592 | tf_op jit(solution)/shard_map/reduce_scatter | solution.py:159
Sparse Core Ops, SparseCore 0:
  51.2 66.8 reduce-scatter.4
  162.9 19.6 reduce-scatter.6
  285.7 88.0 reduce-scatter.8
  377.9 87.9 reduce-scatter.10
where the time goes:
time: 473 us; the launch traced here: 472 us
  waiting for transfers between devices  229 us (48%)
  blocking collectives  145 us (31%)
  matrix products  53.3 us (11%)
  other arithmetic  21.7 us (5%)
  between operations  14 us (3%)
  local copies, waits for them, and re-layouts  5.31 us (1%)
    reduce_scatter x1, waiting for transfers between devices, on_device(): lax.psum_scatter(grad_out_part, 'dp', scatter_dimension=0, tiled=True)  92.1 us
    reduce_scatter x1, waiting for transfers between devices, on_device(): lax.psum_scatter(lax.dot_general(tokens, act_grad, (((0,), (0,)), ((), ()...  85.4 us
    all_gather x1, blocking collectives, on_device(): every_row = lax.all_gather(normed, 'dp', axis=0, tiled=True)  35.3 us
    reduce_scatter x1, waiting for transfers between devices, on_device(): lax.psum_scatter(jnp.concatenate([gate_part, upper_part], axis=1), 'dp',...  32.8 us
    all_gather x1, blocking collectives, on_device(): lax.all_gather(teacher_normalized, 'dp', axis=0, tiled=True)  31.1 us
    all_gather x1, blocking collectives, on_device(): lax.all_gather(hidden, 'dp', axis=0, tiled=True)  31 us
    all_gather x1, blocking collectives, on_device(): lax.all_gather(student_normalized, 'dp', axis=0, tiled=True)  30.9 us
    reduce_scatter x1, waiting for transfers between devices, on_device(): lax.psum_scatter(per_doc, 'section', scatter_dimension=1, tiled=True)  17.8 us
  transfers between devices with their start and end apart: 5, of which 5 were waited for; matrix products, arithmetic and copies ran while one was open for 9% of the time, Pallas kernels for 0%

commit v1 on v0

--- a/solution.py
+++ b/solution.py
@@ -111,7 +111,10 @@
     student_normalized = student_raw / norms
     teacher_normalized = scaled / jnp.sqrt(teacher_total[:, None] + 1e-06)
     all_student_rows, every_teacher = (
-        lax.all_gather(student_normalized, "dp", axis=0, tiled=True),
+        jnp.concatenate(
+            lax.all_to_all(jnp.stack([student_normalized] * lax.axis_size("dp")), "dp", 0, 0),
+            axis=0,
+        ),
         lax.all_gather(teacher_normalized, "dp", axis=0, tiled=True),
     )
     first_row = dp_index * local_docs

time: 473 us -> 456 us (0.964)
  blocking collectives: 145 us -> 114 us
  waiting for transfers between devices: 229 us -> 236 us
  starting transfers between devices: 3.54 us -> 9 us
    all_gather x1 -> x0, blocking collectives: 30.9 us -> none  [on_device(): lax.all_gather(student_normalized, 'dp', axis=0, tiled=True)]
    all_to_all x0 -> x1, waiting for transfers between devices: none -> 7.72 us  [on_device(): lax.all_to_all(jnp.stack([student_normalized] * lax.axis_size('dp')), 'dp...]
    all_to_all x0 -> x1, starting transfers between devices: none -> 5.29 us  [on_device(): lax.all_to_all(jnp.stack([student_normalized] * lax.axis_size('dp')), 'dp...]
  transfers between devices with their start and end apart: 5 -> 6, of which waited for: 5 -> 6; matrix products, arithmetic and copies ran while one was open for 9% -> 9% of each run, Pallas kernels for 0% -> 0%
where the time goes in v1:
time: 456 us; the launch traced here: 455 us
  waiting for transfers between devices  236 us (52%)
  blocking collectives  114 us (25%)
  matrix products  53.3 us (12%)
  other arithmetic  21.7 us (5%)
  between operations  14 us (3%)
  starting transfers between devices  9 us (2%)
  local copies, waits for them, and re-layouts  6.57 us (1%)
    reduce_scatter x1, waiting for transfers between devices, on_device(): lax.psum_scatter(grad_out_part, 'dp', scatter_dimension=0, tiled=True)  92.1 us
    reduce_scatter x1, waiting for transfers between devices, on_device(): lax.psum_scatter(lax.dot_general(tokens, act_grad, (((0,), (0,)), ((), ()...  84.1 us
    all_gather x1, blocking collectives, on_device(): every_row = lax.all_gather(normed, 'dp', axis=0, tiled=True)  35.3 us
    reduce_scatter x1, waiting for transfers between devices, on_device(): lax.psum_scatter(jnp.concatenate([gate_part, upper_part], axis=1), 'dp',...  32.8 us
    all_gather x1, blocking collectives, on_device(): lax.all_gather(teacher_normalized, 'dp', axis=0, tiled=True)  31.1 us
    all_gather x1, blocking collectives, on_device(): lax.all_gather(hidden, 'dp', axis=0, tiled=True)  31 us
    reduce_scatter x1, waiting for transfers between devices, on_device(): lax.psum_scatter(per_doc, 'section', scatter_dimension=1, tiled=True)  17.8 us
    psum x2, blocking collectives, on_device(): emb_sum, teacher_total = lax.psum((partial_emb, teacher_square), 'section')  16.9 us
  transfers between devices with their start and end apart: 6, of which 6 were waited for; matrix products, arithmetic and copies ran while one was open for 9% of the time, Pallas kernels for 0%

profile of v1, /device:TPU:0, one launch (start us, length us, event | category | flops | bytes accessed | tf_op | source)
XLA Modules:
  0.0 454.7 jit_solution(17839511810909865384)
XLA Ops:
  7.2 0.0 copy-start
  7.2 0.0 reduce-scatter.5.cloned.1.call-start
  7.2 1.1 multiply_reduce_fusion
  8.4 0.9 multiply_convert_fusion.5
  9.3 35.3 %all_gather.9 = bf16[64,4096]{1,0:T(8,128)(2,1)} all-gather(bf16[8,4096]{1,0:T(8,128)(2,1)S(1)} %multiply_convert_fusion.5), channel_id=1, replica_groups=mesh['section'=4,'dp'=8] {'dp'}, dimensions={0}, use_global_device_ids=true | all-gather | bytes 589824 | tf_op jit(solution)/shard_map/all_gather | solution.py:67
  44.6 2.6 fusion.12
  47.2 2.6 fusion.14
  49.8 1.3 pad_maximum_fusion
  51.0 0.0 reduce-scatter.5.cloned.1.call-update
  51.1 0.0 copy-start.7
  51.1 0.0 slice-start
  51.1 0.0 copy-start.6
  51.1 4.7 %convert_reduce_fusion = f32[8,512]{1,0:T(8,128)S(1)} fusion(bf16[8,512,1024]{2,1,0:T(8,128)(2,1)} %param.10), kind=kLoop, calls=%fused_computation.2 | loop fusion | flops 8384512 | bytes 8404992 | tf_op jit(solution)/shard_map/reduce_sum | solution.py:12
  55.8 0.0 slice-start.1
  55.8 5.7 %fusion.2 = f32[8,512]{1,0:T(8,128)S(1)} fusion(bf16[8,512,1024]{2,1,0:T(8,128)(2,1)} %param.10, f32[8,512]{1,0:T(8,128)S(1)} %broadcast_multiply_fusion), kind=kLoop, calls=%fused_computation.5 | loop fusion | flops 16773120 | bytes 8421376 | tf_op jit(solution)/shard_map/reduce_sum | solution.py:13
  61.6 0.7 fusion.29
  62.2 0.0 copy-done.6
  62.2 2.8 fusion.4
  65.1 0.0 copy-start.8
  65.1 1.2 fusion.32
  66.3 2.4 copy-done.1
  68.7 16.7 %fusion.8 = (f32[4096,1024]{1,0:T(8,128)}, bf16[4096,1024]{1,0:T(8,128)(2,1)}) fusion(bf16[4096,1024]{1,0:T(8,128)(2,1)S(1)} %bitcast.62, bf16[1024,1024]{1,0:T(8,128)(2,1)S(1)} %copy-done.8), kind=kOutput, calls=%fused_computation.11 | convolution fusion | flops 8636071936 | bytes 35651584 | tf_op jit(solution)/shard_map/dot_general | solution.py:94
  85.3 32.8 %reduce-scatter.5.cloned.1.call-done = f32[8,6144]{1,0:T(8,128)} async-done(((f32[64,6144]{1,0:T(8,128)}), f32[8,6144]{1,0:T(8,128)}) %reduce-scatter.5.cloned.1.call-update) | async-done | bytes 196624 | tf_op jit(solution)/shard_map/reduce_scatter | solution.py:71
  118.1 1.0 fusion.21
  119.1 31.0 %all_gather.10 = bf16[64,3072]{1,0:T(8,128)(2,1)S(1)} all-gather(bf16[8,3072]{1,0:T(8,128)(2,1)S(1)} %fusion.21), channel_id=1, replica_groups=mesh['section'=4,'dp'=8] {'dp'}, dimensions={0}, use_global_device_ids=true | all-gather | bytes 442368 | tf_op jit(solution)/shard_map/all_gather | solution.py:76
  150.1 1.3 convolution_bitcast_fusion
  151.4 3.4 all-to-all-start.1
  154.8 0.0 reduce-scatter.7.cloned.1.call-start
  154.9 4.6 %fusion.30 = f32[8,1,1024]{2,1,0:T(1,128)S(1)} fusion(bf16[8,512,1024]{2,1,0:T(8,128)(2,1)} %bitcast.61, bf16[8,512,1]{1,0,2:T(8,128)(2,1)S(1)} %get-tuple-element.13), kind=kOutput, calls=%fused_computation.61 | convolution fusion | flops 8388608 | bytes 8429568 | tf_op jit(solution)/shard_map/bs,bsf->bf/dot_general | solution.py:101
  159.4 0.7 convert_element_type.50
  160.1 0.7 dynamic_slice.17
  160.8 1.3 all-to-all-done.1
  162.1 0.7 copy-done.3
  162.7 0.0 reduce-scatter.7.cloned.1.call-update
  162.8 2.0 fusion.42
  164.8 17.8 %reduce-scatter.7.cloned.1.call-done = f32[8,1024]{1,0:T(8,128)} async-done(((f32[8,4096]{1,0:T(8,128)}), f32[8,1024]{1,0:T(8,128)}) %reduce-scatter.7.cloned.1.call-update) | async-done | bytes 32784 | tf_op jit(solution)/shard_map/reduce_scatter | solution.py:81
  182.6 0.9 multiply_reduce_fusion.2
  183.5 5.8 %psum.22 = f32[8]{0:T(128)S(1)} all-reduce(f32[8]{0:T(128)S(1)} %get-tuple-element.6), channel_id=1, replica_groups=mesh['section'=4,'dp'=8] {'section'}, use_global_device_ids=true, to_apply=%region_9.10 | all-reduce | flops 8 | bytes 64 | tf_op jit(solution)/shard_map/psum | solution.py:108
  189.3 0.1 multiply_divide_fusion
  189.3 31.1 %all_gather.11 = f32[64,1024]{1,0:T(8,128)S(1)} all-gather(f32[8,1024]{1,0:T(8,128)S(1)} %multiply_divide_fusion), channel_id=1, replica_groups=mesh['section'=4,'dp'=8] {'dp'}, dimensions={0}, use_global_device_ids=true | all-gather | bytes 294912 | tf_op jit(solution)/shard_map/all_gather | solution.py:118
  220.5 0.4 fusion.44
  220.9 11.1 %all-reduce = (f32[8,1024]{1,0:T(8,128)S(1)}, f32[64,64]{0,1:T(8,128)S(1)}) all-reduce(f32[8,1024]{1,0:T(8,128)S(1)} %fusion.42, f32[64,64]{0,1:T(8,128)S(1)} %fusion.44), channel_id=1, replica_groups=mesh['section'=4,'dp'=8] {'section'}, use_global_device_ids=true, to_apply=%region_2.3 | all-reduce | flops 12288 | bytes 98304 | tf_op jit(solution)/shard_map/psum | solution.py:108
  232.0 0.0 copy-start.5
  232.0 0.2 multiply_reduce_fusion.3
  232.2 0.1 broadcast_divide_fusion
  232.3 0.7 stack.2
  233.0 5.3 %all-to-all-start = ((f32[8,8,1024]{2,1,0:T(8,128)}), f32[8,8,1024]{2,1,0:T(8,128)S(1)}, u32[]{:S(2)}, u32[]{:S(2)}) async-start(f32[8,8,1024]{2,1,0:T(8,128)} %stack.2), calls=%async_computation | async-start | bytes 524288 | tf_op jit(solution)/shard_map/all_to_all | solution.py:115
  238.3 0.2 reduce-scatter.9.cloned.1.call-start
  238.6 0.5 log.17
  239.1 7.7 %all-to-all-done = f32[8,8,1024]{2,1,0:T(8,128)S(1)} async-done(((f32[8,8,1024]{2,1,0:T(8,128)}), f32[8,8,1024]{2,1,0:T(8,128)S(1)}, u32[]{:S(2)}, u32[]{:S(2)}) %all-to-all-start) | async-done | bytes 262176 | tf_op jit(solution)/shard_map/all_to_all | solution.py:115
  246.8 0.4 fusion.26
  247.2 1.4 subtract_subtract_fusion
  248.6 0.7 constant_dynamic-slice_fusion
  249.3 0.8 copy.22
  250.1 0.4 multiply_reduce_fusion.1
  250.5 0.1 divide_convert_fusion
  250.6 2.2 convolution_divide_fusion
  252.8 16.3 %fusion.18 = f32[1024,1024]{1,0:T(8,128)} fusion(bf16[8,512,1024]{2,1,0:T(8,128)(2,1)} %copy-done.1, f32[8,512,1024]{2,1,0:T(8,128)} %bitcast.64, f32[8,1024]{1,0:T(8,128)S(1)} %convolution_divide_fusion, f32[8,512]{1,0:T(8,128)} %get-tuple-element.12), kind=kOutput, calls=%fused_computation.24 | convolution fusion | flops 8602517504 | bytes 29409280 | tf_op jit(solution)/shard_map/dot_general | solution.py:155
  269.1 0.0 reduce-scatter.9.cloned.1.call-update
  269.2 0.0 reduce-scatter.11.cloned.1.call-start
  269.2 2.8 fusion.40
  272.0 0.0 reduce-scatter.11.cloned.1.call-update
  272.0 84.1 %reduce-scatter.9.cloned.1.call-done = f32[128,1024]{1,0:T(8,128)} async-done(((f32[1024,1024]{1,0:T(8,128)}), f32[128,1024]{1,0:T(8,128)}) %reduce-scatter.9.cloned.1.call-update) | async-done | bytes 524304 | tf_op jit(solution)/shard_map/reduce_scatter | solution.py:154
  356.1 92.1 %reduce-scatter.11.cloned.1.call-done = f32[128,1024]{1,0:T(8,128)} async-done(((f32[1024,1024]{1,0:T(8,128)}), f32[128,1024]{1,0:T(8,128)}) %reduce-scatter.11.cloned.1.call-update) | async-done | bytes 524304 | tf_op jit(solution)/shard_map/reduce_scatter | solution.py:162
  (22 shorter events, 0.1 us)
Async XLA Ops:
  7.2 142.9 %copy-start = (bf16[3072,512]{1,0:T(8,128)(2,1)S(1)}, bf16[3072,512]{1,0:T(8,128)(2,1)}, u32[]{:S(2)}) copy-start(bf16[3072,512]{1,0:T(8,128)(2,1)} %param.18) | copy-start | bytes 9437188
  7.2 110.9 %reduce-scatter.5.cloned.1.call-start = ((), (), s32[]{:S(2)}) async-start(), calls=%async_computation.6 | async-start | bytes 1769472 | tf_op jit(solution)/shard_map/reduce_scatter | solution.py:71
  51.1 10.5 %copy-start.7 = (s32[8]{0:T(128)S(1)}, s32[8]{0:T(128)}, u32[]{:S(2)}) copy-start(s32[8]{0:T(128)} %param.11) | copy-start | bytes 100
  51.1 11.2 %slice-start = ((s8[8388608]{0:T(1024)(128)(4,1)}), s8[4194304]{0:T(1024)(128)(4,1)S(1)}, s32[]{:S(2)}) async-start(s8[8388608]{0:T(1024)(128)(4,1)} %bitcast.59), calls=%async_computation.10 | async-start | bytes 8388608
  51.1 11.2 %copy-start.6 = (f32[1024]{0:T(1024)S(1)}, f32[1024]{0:T(1024)}, u32[]{:S(2)}) copy-start(f32[1024]{0:T(1024)} %param.12) | copy-start | bytes 12292
  55.8 6.4 %slice-start.1 = ((s8[8388608]{0:T(1024)(128)(4,1)}), s8[4194304]{0:T(1024)(128)(4,1)S(1)}, s32[]{:S(2)}) async-start(s8[8388608]{0:T(1024)(128)(4,1)} %bitcast.59), calls=%async_computation.11 | async-start | bytes 8388608
  65.1 3.6 copy-start.1
  65.1 3.6 copy-start.8
  85.3 74.1 %copy-start.2 = (bf16[8,4096]{1,0:T(8,128)(2,1)S(1)}, bf16[8,4096]{1,0:T(8,128)(2,1)}, u32[]{:S(2)}) copy-start(bf16[8,4096]{1,0:T(8,128)(2,1)} %param.15) | copy-start | bytes 196612
  151.4 10.7 %all-to-all-start.1 = ((f32[8,8,512]{2,1,0:T(8,128)}), f32[8,8,512]{2,1,0:T(8,128)S(1)}, u32[]{:S(2)}, u32[]{:S(2)}) async-start(f32[8,8,512]{2,1,0:T(8,128)} %convolution_bitcast_fusion), calls=%async_computation.2 | async-start | bytes 262144 | tf_op jit(solution)/shard_map/all_to_all | solution.py:80
  154.8 27.8 %reduce-scatter.7.cloned.1.call-start = ((), (), s32[]{:S(2)}) async-start(), calls=%async_computation.7 | async-start | bytes 163840 | tf_op jit(solution)/shard_map/reduce_scatter | solution.py:81
  162.1 0.7 copy-start.3
  183.5 85.7 %copy-start.4 = (f32[8,1024]{1,0:T(8,128)}, f32[8,1024]{1,0:T(8,128)S(1)}, u32[]{:S(2)}) copy-start(f32[8,1024]{1,0:T(8,128)S(1)} %get-tuple-element.7) | copy-start | bytes 98308
  232.0 15.3 %copy-start.5 = (f32[64,64]{0,1:T(8,128)}, f32[64,64]{0,1:T(8,128)S(1)}, u32[]{:S(2)}) copy-start(f32[64,64]{0,1:T(8,128)S(1)} %get-tuple-element.5) | copy-start | bytes 49156
  233.0 13.8 %all-to-all-start = ((f32[8,8,1024]{2,1,0:T(8,128)}), f32[8,8,1024]{2,1,0:T(8,128)S(1)}, u32[]{:S(2)}, u32[]{:S(2)}) async-start(f32[8,8,1024]{2,1,0:T(8,128)} %stack.2), calls=%async_computation | async-start | bytes 524288 | tf_op jit(solution)/shard_map/all_to_all | solution.py:115
  238.3 117.8 %reduce-scatter.9.cloned.1.call-start = ((), (), s32[]{:S(2)}) async-start(), calls=%async_computation.8 | async-start | bytes 4718592 | tf_op jit(solution)/shard_map/reduce_scatter | solution.py:154
  269.2 179.0 %reduce-scatter.11.cloned.1.call-start = ((), (), s32[]{:S(2)}) async-start(), calls=%async_computation.9 | async-start | bytes 4718592 | tf_op jit(solution)/shard_map/reduce_scatter | solution.py:162
Sparse Core Ops, SparseCore 0:
  51.2 66.8 reduce-scatter.4
  162.9 19.6 reduce-scatter.6
  269.3 86.7 reduce-scatter.8
  360.2 87.9 reduce-scatter.10
